TPU v7x, 32 devices: a whole 2x2x4 slice. The times are simulated.
32 devices in a mesh: det: 8 (over y, x, core), bm: 4 (over z).
Axes of the slice: x: 2, y: 2, z: 4, core: 2. Of those that a mesh axis runs over, the one named last changes fastest.
Arguments:
- sky_alm: bfloat16 [2, 3, 16, 128], P(None, None, 'det'), may hold values from -6 to 6
- beam_blm: bfloat16 [2, 3, 16, 128], P(None, None, 'bm'), may hold values from -2.5 to 2.5
- wigner: bfloat16 [32, 16, 16, 128], P('det', None, 'bm'), may hold values from -0.03125 to 0.03125
- theta_index: int32 [128, 256], P('det'), may hold values from 0 to 3
- phi_index: int32 [128, 256], P('det'), may hold values from 0 to 16383
- psi_index: int32 [128, 256], P('det'), may hold values from 0 to 31
Outputs:
- tod: float32 [128, 256], P('det', 'bm')
All inputs are finite; a program needn't handle non-finite values.
Results may differ from a plain program's by a relative error of at most 0.0029.
Values may be sent and summed in bfloat16 or wider, within the bound.
A program may use at most 64 MiB of HBM per device.

v0:
```python
import functools
import math

import jax
import jax.numpy as jnp
from jax import lax
from jax.experimental import pallas as pl
from jax.experimental.pallas import tpu as pltpu
from jax.sharding import PartitionSpec as P

NPHI = 16384
NPSI = 32

TWO_PI = 2.0 * math.pi
LANES = 128
ROWS = 8
F32 = jnp.float32
BF16 = jnp.bfloat16
MESH = pl.DeviceIdType.MESH


def cos_on_grid(step, grid):
    shift = (grid // 4).bit_length() - 1
    turn = (step + grid // 8) >> shift
    x = (step - (turn << shift)).astype(F32) * (TWO_PI / grid)
    x2 = x * x
    c = 1.0 + x2 * (-0.5 + x2 * (1 / 24 + x2 * (-1 / 720 + x2 * (1 / 40320))))
    s = x * (1.0 + x2 * (-1 / 6 + x2 * (1 / 120 + x2 * (-1 / 5040 + x2 * (1 / 362880)))))
    odd = (turn & 1) == 1
    value = jnp.where(odd, -s, c)
    return jnp.where((turn & 2) == 2, -value, value)


def partner(me, flip, n):
    out, bit = 0, 1
    while bit < n:
        digit = (me // bit) % 2
        out = out + bit * ((1 - digit) if flip & bit else digit)
        bit *= 2
    return out


def rows_of(values, groups, width):
    return jnp.concatenate([values[j * ROWS : (j + 1) * ROWS] for j in range(groups)], axis=1)


def kernel(
    n_det, n_bm,
    sky_hbm, beam_hbm, wig_hbm, theta_hbm, phi_hbm, psi_hbm, out_ref,
    sky_all, beam, wig, index, wide, feat, phase, cube_all,
    local_sem, sky_send, sky_recv, cube_send, cube_recv, ready,
):
    det = lax.axis_index("det")
    bm = lax.axis_index("bm")
    local = [
        pltpu.make_async_copy(sky_hbm, sky_all.at[det], local_sem.at[0]),
        pltpu.make_async_copy(beam_hbm, beam, local_sem.at[1]),
        pltpu.make_async_copy(wig_hbm, wig, local_sem.at[2]),
        pltpu.make_async_copy(theta_hbm, index.at[0], local_sem.at[3]),
        pltpu.make_async_copy(phi_hbm, index.at[1], local_sem.at[4]),
        pltpu.make_async_copy(psi_hbm, index.at[2], local_sem.at[5]),
    ]
    for copy in local:
        copy.start()
    barrier = pltpu.get_barrier_semaphore()
    for flip in range(1, n_det):
        pl.semaphore_signal(
            barrier, inc=1, device_id=(partner(det, flip, n_det), bm), device_id_type=MESH
        )
    relayed = n_bm == 4
    greeted = (1, 2) if relayed else range(1, n_bm)
    for flip in greeted:
        pl.semaphore_signal(
            barrier, inc=1, device_id=(det, partner(bm, flip, n_bm)), device_id_type=MESH
        )
    local[0].wait()
    pl.semaphore_wait(barrier, n_det - 1 + len(greeted))
    sends = []
    for flip in range(n_det - 1, 0, -1):
        copy = pltpu.make_async_remote_copy(
            src_ref=sky_all.at[det],
            dst_ref=sky_all.at[det],
            send_sem=sky_send.at[flip],
            recv_sem=sky_recv.at[flip],
            device_id=(partner(det, flip, n_det), bm),
            device_id_type=MESH,
        )
        copy.start()
        sends.append(copy)
    if relayed:
        pl.semaphore_signal(
            ready, inc=1, device_id=(det, partner(bm, 1, n_bm)), device_id_type=MESH
        )
    for copy in local[1:]:
        copy.wait()

    cycles, flat, band = wig.shape
    planes = beam.shape[2]
    modes = flat // planes
    owned = sky_all.shape[3]
    pairs = cycles * planes
    depth = 2 * pairs
    per_tile = LANES // (2 * depth)
    tile_modes = per_tile * ROWS
    tiles = modes // tile_modes
    dets, samples = index.shape[1:]
    width = samples // n_bm
    groups = dets // ROWS

    for g in range(cycles):
        wide[g] = wig[g].astype(F32)

    def mine(values):
        own = values[:, :width]
        for i in range(1, n_bm):
            own = jnp.where(bm == i, values[:, i * width : (i + 1) * width], own)
        return rows_of(own, groups, width)

    theta, phi, psi = mine(index[0]), mine(index[1]), mine(index[2])
    span = groups * width
    k_rows = n_bm * depth
    row = lax.broadcasted_iota(jnp.int32, (k_rows, span), 0)
    source = 0
    for flip in range(n_bm):
        source = jnp.where(row // depth == flip, partner(bm, flip, n_bm), source)
    plane = source * planes + row % planes
    cycle = (row // planes) % cycles
    quarter = ((row // pairs) % 2) * (3 * NPSI // 4)
    m_rows = 2 * modes
    mrow = lax.broadcasted_iota(jnp.int32, (m_rows, span), 0)
    mode = (mrow // (2 * tile_modes)) * tile_modes + mrow % tile_modes
    mquarter = ((mrow // tile_modes) % 2) * (NPHI // 4)
    for j in range(ROWS):
        at = pl.ds(j * span, span)
        step = (plane * psi[j : j + 1] + quarter) & (NPSI - 1)
        value = jnp.where(cycle == theta[j : j + 1], cos_on_grid(step, NPSI), 0.0)
        high = value.astype(BF16)
        feat[:k_rows, at] = high
        feat[k_rows:, at] = (value - high.astype(F32)).astype(BF16)
        step = (mode * phi[j : j + 1] + mquarter) & (NPHI - 1)
        phase[:, at] = cos_on_grid(step, NPHI)

    for copy in sends:
        copy.wait_recv()

    lane = lax.broadcasted_iota(jnp.int32, (ROWS, LANES), 1)
    imag_row = (lane // (depth * per_tile)) % 2
    sin_column = (lane // pairs) % 2
    part = (imag_row + sin_column) % 2
    code = ((lane // depth) % per_tile * 2 + part) * pairs + lane % pairs
    sign = jnp.where((imag_row == 0) & (sin_column == 1), -1.0, 1.0)
    slots = tile_modes // owned
    for t in range(tiles):
        sky = [
            [
                sky_all[t * slots : (t + 1) * slots, r, c].astype(F32).reshape(tile_modes, band)
                for c in range(3)
            ]
            for r in range(2)
        ]
        packed = jnp.zeros((ROWS, LANES), F32)
        for h in range(per_tile):
            for p in range(planes):
                re = im = 0.0
                for c in range(3):
                    s0 = sky[0][c][h * ROWS : (h + 1) * ROWS]
                    s1 = sky[1][c][h * ROWS : (h + 1) * ROWS]
                    b0 = beam[0, c, p : p + 1].astype(F32)
                    b1 = beam[1, c, p : p + 1].astype(F32)
                    re = re + (s0 * b0 - s1 * b1)
                    im = im + (s0 * b1 + s1 * b0)
                re = re.astype(BF16).astype(F32)
                im = im.astype(BF16).astype(F32)
                first = (t * tile_modes + h * ROWS) * planes + p
                for g in range(cycles):
                    w = wide[g, pl.ds(first, ROWS, stride=planes)]
                    for k, spectra in enumerate((re, im)):
                        total = jnp.sum(w * spectra, axis=1, keepdims=True)
                        where = (h * 2 + k) * pairs + g * planes + p
                        packed = jnp.where(code == where, total, packed)
        cube_all[0, t] = packed * sign

    later = []
    if relayed:
        pl.semaphore_wait(ready, 1)
    for flip in range(n_bm - 1, 0, -1):
        copy = pltpu.make_async_remote_copy(
            src_ref=cube_all.at[0],
            dst_ref=cube_all.at[flip],
            send_sem=cube_send.at[flip],
            recv_sem=cube_recv.at[flip],
            device_id=(det, partner(bm, flip, n_bm)),
            device_id_type=MESH,
        )
        copy.start()
        later.append(copy)
    for copy in later:
        copy.wait_recv()

    blocks = []
    for t in range(tiles):
        parts = [cube_all[s, t] for s in range(n_bm)]
        for q in range(2 * per_tile):
            blocks.append(
                jnp.concatenate([x[:, q * depth : (q + 1) * depth] for x in parts], axis=1)
            )
    left = jnp.concatenate(blocks, axis=0)
    high = left.astype(BF16)
    low = (left - high.astype(F32)).astype(BF16)
    both = jnp.concatenate(
        [jnp.concatenate([high, high], axis=1), jnp.concatenate([low, low], axis=1)], axis=0
    )
    y = jnp.dot(both, feat[...], preferred_element_type=F32)
    z = (y[:m_rows] + y[m_rows:]) * phase[...]
    total = jnp.sum(z, axis=0, keepdims=True)
    for j in range(ROWS):
        for i in range(groups):
            at = j * span + i * width
            out_ref[pl.ds(i * ROWS + j, 1), :] = total[:, at : at + width]

    for copy in sends + later:
        copy.wait_send()


def on_device(sky_alm, beam_blm, wigner, theta_index, phi_index, psi_index):
    n_det, n_bm = lax.axis_size("det"), lax.axis_size("bm")
    cycles, modes, planes, band = wigner.shape
    dets, samples = theta_index.shape
    width = samples // n_bm
    span = dets // ROWS * width
    depth = 2 * cycles * planes
    tiles = modes * 2 * depth // (ROWS * LANES)
    any_space = pl.BlockSpec(memory_space=pl.ANY)
    out = pl.pallas_call(
        functools.partial(kernel, n_det, n_bm),
        out_shape=pltpu.VMEM((dets, width), F32),
        in_specs=[any_space] * 6,
        out_specs=pl.BlockSpec(memory_space=pltpu.VMEM),
        scratch_shapes=[
            pltpu.VMEM((n_det, *sky_alm.shape), BF16),
            pltpu.VMEM(beam_blm.shape, BF16),
            pltpu.VMEM((cycles, modes * planes, band), BF16),
            pltpu.VMEM((3, dets, samples), jnp.int32),
            pltpu.VMEM((cycles, modes * planes, band), F32),
            pltpu.VMEM((2 * n_bm * depth, ROWS * span), BF16),
            pltpu.VMEM((2 * modes, ROWS * span), F32),
            pltpu.VMEM((n_bm, tiles, ROWS, LANES), F32),
            pltpu.SemaphoreType.DMA((6,)),
            pltpu.SemaphoreType.DMA((n_det,)),
            pltpu.SemaphoreType.DMA((n_det,)),
            pltpu.SemaphoreType.DMA((n_bm,)),
            pltpu.SemaphoreType.DMA((n_bm,)),
            pltpu.SemaphoreType.REGULAR,
        ],
        compiler_params=pltpu.CompilerParams(collective_id=0, has_side_effects=True),
    )(
        sky_alm,
        beam_blm,
        wigner.reshape(cycles, modes * planes, band),
        theta_index,
        phi_index,
        psi_index,
    )
    return out


def solution(mesh):
    placed = (
        P(None, None, "det", None),
        P(None, None, "bm", None),
        P("det", None, "bm", None),
        P("det", None),
        P("det", None),
        P("det", None),
    )
    return jax.shard_map(
        on_device, mesh=mesh, in_specs=placed, out_specs=P("det", "bm"), check_vma=False
    )
```

profile of v0, /device:TPU:0, one launch (start us, length us, event | category | flops | bytes accessed | tf_op | source)
XLA Modules:
  0.0 12.9 jit_solution(3180615980578529281)
XLA Ops:
  0.0 12.3 %shard_map.64 = f32[16,64]{1,0:T(8,128)S(1)} custom-call(bf16[2,3,2,128]{3,2,1,0:T(2,128)(2,1)} %sky_hbm.1, bf16[2,3,4,128]{3,2,1,0:T(4,128)(2,1)} %beam_hbm.1, bf16[4,64,128]{2,1,0:T(8,128)(2,1)} %bitcast.1, s32[16,256]{1,0:T(8,128)} %theta_hbm.1, s32[16,256]{1,0:T(8,128)} %phi_hbm.1, s32[16,256]{1,0:T(8,128)} %psi_hbm.1), custom_call_target="tpu_custom_call" | custom-call | tf_op jit(solution)/shard_map/pallas_call | solution.py:234
  12.3 0.6 %copy.8 = f32[16,64]{1,0:T(8,128)} copy(f32[16,64]{1,0:T(8,128)S(1)} %shard_map.64) | data formatting | bytes 8192
where the time goes:
time: 13.1 us; the launch traced here: 12.9 us
  Pallas kernels  12.3 us (94%)
  local copies, waits for them, and re-layouts  0.6 us (5%)
    pallas_call x1, Pallas kernels, on_device(): pl.pallas_call(functools.partial(kernel, n_det, n_bm), out_shape=pltpu.VM...  12.3 us
    unnamed x1, local copies, waits for them, and re-layouts  0.6 us

commit v1 on v0

v1 whole, which is shorter than its diff:
```python
import functools
import math

import jax
import jax.numpy as jnp
from jax import lax
from jax.experimental import pallas as pl
from jax.experimental.pallas import tpu as pltpu
from jax.sharding import PartitionSpec as P

NPHI = 16384
NPSI = 32

TWO_PI = 2.0 * math.pi
LANES = 128
ROWS = 8
PUSH_BYTES = 1 << 18
F32 = jnp.float32
BF16 = jnp.bfloat16
MESH = pl.DeviceIdType.MESH


def cos_on_grid(step, grid):
    shift = (grid // 4).bit_length() - 1
    turn = (step + grid // 8) >> shift
    x = (step - (turn << shift)).astype(F32) * (TWO_PI / grid)
    x2 = x * x
    c = 1.0 + x2 * (-0.5 + x2 * (1 / 24 + x2 * (-1 / 720 + x2 * (1 / 40320))))
    s = x * (1.0 + x2 * (-1 / 6 + x2 * (1 / 120 + x2 * (-1 / 5040 + x2 * (1 / 362880)))))
    odd = (turn & 1) == 1
    value = jnp.where(odd, -s, c)
    return jnp.where((turn & 2) == 2, -value, value)


def partner(me, flip, n):
    out, bit = 0, 1
    while bit < n:
        digit = (me // bit) % 2
        out = out + bit * ((1 - digit) if flip & bit else digit)
        bit *= 2
    return out


def rows_of(values, groups, width):
    return jnp.concatenate([values[j * ROWS : (j + 1) * ROWS] for j in range(groups)], axis=1)


def pushed(even, n_bm, source, target):
    return (even & (source > target) & (target == 0)) | (source - target >= n_bm - 1)


def kernel(
    n_det, n_bm, cycles, pushes,
    sky_hbm, beam_hbm, wig_hbm, theta_hbm, phi_hbm, psi_hbm, out_ref,
    sky_all, slab, index, sky_wide, wide, feat, phase, cube_all,
    local_sem, sky_sem, col_send, col_recv, ok, hello,
):
    det = lax.axis_index("det")
    bm = lax.axis_index("bm")
    even = det % 2 == 0
    pair = det // 2
    buddy = det + 1 - 2 * (det % 2)
    n_pairs = n_det // 2

    rows, band = slab.shape[1:]
    beam_rows = beam_hbm.shape[0]
    wig_rows = rows - beam_rows
    planes = beam_rows // 6
    flat = wig_rows // cycles
    modes = flat // planes
    owned = sky_all.shape[3]
    pairs = cycles * planes
    depth = 2 * pairs
    per_tile = LANES // (2 * depth)
    tile_modes = per_tile * ROWS
    tiles = modes // tile_modes
    dets, samples = index.shape[1:]
    width = samples // n_bm
    groups = dets // ROWS

    pltpu.make_async_copy(sky_hbm, sky_all.at[det], local_sem.at[0]).start()
    for g in range(cycles):
        part = pl.ds(g * flat, flat)
        pltpu.make_async_copy(wig_hbm.at[part], slab.at[bm, part], local_sem.at[1]).start()
    pltpu.make_async_copy(beam_hbm, slab.at[bm, pl.ds(wig_rows, beam_rows)], local_sem.at[1]).start()
    pltpu.make_async_copy(theta_hbm, index.at[0], local_sem.at[2]).start()
    pltpu.make_async_copy(phi_hbm, index.at[1], local_sem.at[2]).start()
    pltpu.make_async_copy(psi_hbm, index.at[2], local_sem.at[2]).start()

    barrier = pltpu.get_barrier_semaphore()

    def greet(semaphore, to_det, to_bm):
        pl.semaphore_signal(semaphore, inc=1, device_id=(to_det, to_bm), device_id_type=MESH)

    greet(barrier, buddy, bm)
    for z in range(1, n_bm):
        @pl.when(bm < z)
        def _():
            greet(barrier, 2 * pair + 1, z)
    for k in range(1, n_pairs):
        greet(barrier, 2 * ((pair + k) % n_pairs), bm)

    def push_to(z):
        return pltpu.make_async_remote_copy(
            src_ref=slab.at[bm], dst_ref=slab.at[bm],
            send_sem=col_send.at[z], recv_sem=col_recv.at[bm],
            device_id=(det, z), device_id_type=MESH,
        )

    def cube_to(z):
        return pltpu.make_async_remote_copy(
            src_ref=cube_all.at[bm], dst_ref=cube_all.at[bm],
            send_sem=col_send.at[z], recv_sem=col_recv.at[bm],
            device_id=(det, z), device_id_type=MESH,
        )

    def landing(buffer, z):
        return pltpu.make_async_remote_copy(
            src_ref=buffer.at[z], dst_ref=buffer.at[z],
            send_sem=col_send.at[z], recv_sem=col_recv.at[z],
            device_id=(det, z), device_id_type=MESH,
        )

    @pl.when(jnp.logical_not(even))
    def _():
        pl.semaphore_wait(barrier, 1 + 2 * bm)
        greet(ok, buddy, bm)

    def share_sky():
        @pl.when(even)
        def _():
            pl.semaphore_wait(barrier, n_det - 1)
            greet(ok, buddy, bm)

        @pl.when(jnp.logical_not(even))
        def _():
            pl.semaphore_wait(ok, 1)

        pltpu.make_async_copy(sky_hbm, sky_all.at[det], local_sem.at[0]).wait()
        for flip in range(n_det - 1, 0, -1):
            pltpu.make_async_remote_copy(
                src_ref=sky_all.at[det], dst_ref=sky_all.at[det],
                send_sem=sky_sem.at[0], recv_sem=sky_sem.at[1],
                device_id=(partner(det, flip, n_det), bm), device_id_type=MESH,
            ).start()

    def share_slab():
        @pl.when(even)
        def _():
            pl.semaphore_wait(ok, 1)

        for z in range(n_bm - 1):
            @pl.when(bm > z)
            def _():
                greet(hello, det, z)
        pltpu.make_async_copy(slab.at[bm], slab.at[bm], local_sem.at[1]).wait()
        if pushes:
            for z in range(n_bm - 1):
                @pl.when(pushed(even, n_bm, bm, z))
                def _():
                    push_to(z).start()

    last = pair == n_pairs - 1

    @pl.when(last)
    def _():
        share_sky()

    share_slab()

    @pl.when(jnp.logical_not(last))
    def _():
        share_sky()

    others = sky_all.at[pl.ds(0, n_det - 1)]
    skies = pltpu.make_async_remote_copy(
        src_ref=others, dst_ref=others,
        send_sem=sky_sem.at[0], recv_sem=sky_sem.at[1],
        device_id=(buddy, bm), device_id_type=MESH,
    )
    pltpu.make_async_copy(index, index, local_sem.at[2]).wait()

    def widen(z):
        for g in range(cycles):
            wide[g] = slab[z, pl.ds(g * flat, flat)].astype(F32)

    def mine(values):
        own = values[:, :width]
        for i in range(1, n_bm):
            own = jnp.where(bm == i, values[:, i * width : (i + 1) * width], own)
        return rows_of(own, groups, width)

    theta, phi, psi = mine(index[0]), mine(index[1]), mine(index[2])
    span = groups * width
    k_rows = n_bm * depth
    row = lax.broadcasted_iota(jnp.int32, (k_rows, span), 0)
    plane = row // depth * planes + row % planes
    cycle = (row // planes) % cycles
    quarter = ((row // pairs) % 2) * (3 * NPSI // 4)
    m_rows = 2 * modes
    mrow = lax.broadcasted_iota(jnp.int32, (m_rows, span), 0)
    mode = (mrow // (2 * tile_modes)) * tile_modes + mrow % tile_modes
    mquarter = ((mrow // tile_modes) % 2) * (NPHI // 4)
    for j in range(ROWS):
        at = pl.ds(j * span, span)
        step = (plane * psi[j : j + 1] + quarter) & (NPSI - 1)
        value = jnp.where(cycle == theta[j : j + 1], cos_on_grid(step, NPSI), 0.0)
        high = value.astype(BF16)
        feat[:k_rows, at] = high
        feat[k_rows:, at] = (value - high.astype(F32)).astype(BF16)
        step = (mode * phi[j : j + 1] + mquarter) & (NPHI - 1)
        phase[:, at] = cos_on_grid(step, NPHI)

    widen(bm)
    skies.wait_recv()

    slots = tile_modes // owned
    for t in range(tiles):
        for r in range(2):
            for c in range(3):
                sky_wide[r, c, pl.ds(t * tile_modes, tile_modes)] = (
                    sky_all[t * slots : (t + 1) * slots, r, c].astype(F32).reshape(tile_modes, band)
                )

    lane = lax.broadcasted_iota(jnp.int32, (ROWS, LANES), 1)
    imag_row = (lane // (depth * per_tile)) % 2
    sin_column = (lane // pairs) % 2
    part = (imag_row + sin_column) % 2
    code = ((lane // depth) % per_tile * 2 + part) * pairs + lane % pairs
    sign = jnp.where((imag_row == 0) & (sin_column == 1), -1.0, 1.0)

    def profile(z):
        beam = slab[z, pl.ds(wig_rows, beam_rows)].astype(F32)
        for t in range(tiles):
            packed = jnp.zeros((ROWS, LANES), F32)
            for h in range(per_tile):
                at = t * tile_modes + h * ROWS
                sky = [[sky_wide[r, c, pl.ds(at, ROWS)] for c in range(3)] for r in range(2)]
                for p in range(planes):
                    re = im = 0.0
                    for c in range(3):
                        b0 = beam[c * planes + p : c * planes + p + 1]
                        b1 = beam[(3 + c) * planes + p : (3 + c) * planes + p + 1]
                        re = re + (sky[0][c] * b0 - sky[1][c] * b1)
                        im = im + (sky[0][c] * b1 + sky[1][c] * b0)
                    re = re.astype(BF16).astype(F32)
                    im = im.astype(BF16).astype(F32)
                    for g in range(cycles):
                        w = wide[g, pl.ds(at * planes + p, ROWS, stride=planes)]
                        for k, spectra in enumerate((re, im)):
                            total = jnp.sum(w * spectra, axis=1, keepdims=True)
                            where = (h * 2 + k) * pairs + g * planes + p
                            packed = jnp.where(code == where, total, packed)
            cube_all[z, t] = packed * sign

    profile(bm)

    @pl.when(bm < n_bm - 1)
    def _():
        pl.semaphore_wait(hello, n_bm - 1 - bm)

    def by_cube(source, target):
        apart = source != target
        return apart & jnp.logical_not(pushed(even, n_bm, source, target)) if pushes else apart

    for z in range(n_bm - 1, -1, -1):
        @pl.when(by_cube(bm, z))
        def _():
            cube_to(z).start()

    for z in range(n_bm):
        @pl.when(by_cube(z, bm))
        def _():
            landing(cube_all, z).wait_recv()
        if pushes and z > 0:
            @pl.when(pushed(even, n_bm, z, bm))
            def _():
                landing(slab, z).wait_recv()
                widen(z)
                profile(z)

    blocks = []
    for t in range(tiles):
        parts = [cube_all[s, t] for s in range(n_bm)]
        for q in range(2 * per_tile):
            blocks.append(
                jnp.concatenate([x[:, q * depth : (q + 1) * depth] for x in parts], axis=1)
            )
    left = jnp.concatenate(blocks, axis=0)
    high = left.astype(BF16)
    low = (left - high.astype(F32)).astype(BF16)
    both = jnp.concatenate(
        [jnp.concatenate([high, high], axis=1), jnp.concatenate([low, low], axis=1)], axis=0
    )
    y = jnp.dot(both, feat[...], preferred_element_type=F32)
    z = (y[:m_rows] + y[m_rows:]) * phase[...]
    total = jnp.sum(z, axis=0, keepdims=True)
    for j in range(ROWS):
        for i in range(groups):
            at = j * span + i * width
            out_ref[pl.ds(i * ROWS + j, 1), :] = total[:, at : at + width]

    skies.wait_send()
    for z in range(n_bm):
        @pl.when(by_cube(bm, z))
        def _():
            cube_to(z).wait_send()
        if pushes and z < n_bm - 1:
            @pl.when(pushed(even, n_bm, bm, z))
            def _():
                push_to(z).wait_send()


def on_device(sky_alm, beam_blm, wigner, theta_index, phi_index, psi_index):
    n_det, n_bm = lax.axis_size("det"), lax.axis_size("bm")
    cycles, modes, planes, band = wigner.shape
    dets, samples = theta_index.shape
    width = samples // n_bm
    span = dets // ROWS * width
    depth = 2 * cycles * planes
    tiles = modes * 2 * depth // (ROWS * LANES)
    beam_rows = 6 * planes
    wig_rows = cycles * modes * planes
    pushes = 2 * wig_rows * band <= PUSH_BYTES
    any_space = pl.BlockSpec(memory_space=pl.ANY)
    return pl.pallas_call(
        functools.partial(kernel, n_det, n_bm, cycles, pushes),
        out_shape=pltpu.VMEM((dets, width), F32),
        in_specs=[any_space] * 6,
        out_specs=pl.BlockSpec(memory_space=pltpu.VMEM),
        scratch_shapes=[
            pltpu.VMEM((n_det, *sky_alm.shape), BF16),
            pltpu.VMEM((n_bm, wig_rows + beam_rows, band), BF16),
            pltpu.VMEM((3, dets, samples), jnp.int32),
            pltpu.VMEM((2, 3, modes, band), F32),
            pltpu.VMEM((cycles, modes * planes, band), F32),
            pltpu.VMEM((2 * n_bm * depth, ROWS * span), BF16),
            pltpu.VMEM((2 * modes, ROWS * span), F32),
            pltpu.VMEM((n_bm, tiles, ROWS, LANES), F32),
            pltpu.SemaphoreType.DMA((3,)),
            pltpu.SemaphoreType.DMA((2,)),
            pltpu.SemaphoreType.DMA((n_bm,)),
            pltpu.SemaphoreType.DMA((n_bm,)),
            pltpu.SemaphoreType.REGULAR,
            pltpu.SemaphoreType.REGULAR,
        ],
        compiler_params=pltpu.CompilerParams(collective_id=0, has_side_effects=True),
    )(
        sky_alm,
        beam_blm.reshape(beam_rows, band),
        wigner.reshape(wig_rows, band),
        theta_index,
        phi_index,
        psi_index,
    )


def solution(mesh):
    placed = (
        P(None, None, "det", None),
        P(None, None, "bm", None),
        P("det", None, "bm", None),
        P("det", None),
        P("det", None),
        P("det", None),
    )
    return jax.shard_map(
        on_device, mesh=mesh, in_specs=placed, out_specs=P("det", "bm"), check_vma=False
    )
```

time: 13.1 us -> 10.7 us (0.82)
  the two profiles are of different devices: /device:TPU:0 before, /device:TPU:1 now
where the time goes in v1:
time: 10.7 us; the launch traced here: 10.5 us
  Pallas kernels  9.94 us (93%)
  local copies, waits for them, and re-layouts  0.6 us (6%)
    pallas_call x1, Pallas kernels, on_device(): pl.pallas_call(functools.partial(kernel, n_det, n_bm, cycles, pushes), ou...  9.94 us
    unnamed x1, local copies, waits for them, and re-layouts  0.6 us

profile of v1, /device:TPU:1, one launch (start us, length us, event | category | flops | bytes accessed | tf_op | source)
XLA Modules:
  0.0 10.5 jit_solution(17044992803677584155)
XLA Ops:
  0.0 9.9 %shard_map.64 = f32[16,64]{1,0:T(8,128)S(1)} custom-call(bf16[2,3,2,128]{3,2,1,0:T(2,128)(2,1)} %sky_hbm.1, bf16[24,128]{1,0:T(8,128)(2,1)} %bitcast.3, bf16[256,128]{1,0:T(8,128)(2,1)} %bitcast.2, s32[16,256]{1,0:T(8,128)} %theta_hbm.1, s32[16,256]{1,0:T(8,128)} %phi_hbm.1, s32[16,256]{1,0:T(8,128)} %psi_hbm.1), custom_call_target="tpu_custom_call" | custom-call | tf_op jit(solution)/shard_map/pallas_call | solution.py:326
  9.9 0.6 %copy.8 = f32[16,64]{1,0:T(8,128)} copy(f32[16,64]{1,0:T(8,128)S(1)} %shard_map.64) | data formatting | bytes 8192

commit v2 on v1

--- a/solution.py
+++ b/solution.py
@@ -52,7 +52,7 @@
 def kernel(
     n_det, n_bm, cycles, pushes,
     sky_hbm, beam_hbm, wig_hbm, theta_hbm, phi_hbm, psi_hbm, out_ref,
-    sky_all, slab, index, sky_wide, wide, feat, phase, cube_all,
+    sky_all, slab, index, sky_wide, wide, feat, phase, cube_all, left,
     local_sem, sky_sem, col_send, col_recv, ok, hello,
 ):
     det = lax.axis_index("det")
@@ -205,9 +205,7 @@
         at = pl.ds(j * span, span)
         step = (plane * psi[j : j + 1] + quarter) & (NPSI - 1)
         value = jnp.where(cycle == theta[j : j + 1], cos_on_grid(step, NPSI), 0.0)
-        high = value.astype(BF16)
-        feat[:k_rows, at] = high
-        feat[k_rows:, at] = (value - high.astype(F32)).astype(BF16)
+        feat[:, at] = value.astype(BF16)
         step = (mode * phi[j : j + 1] + mquarter) & (NPHI - 1)
         phase[:, at] = cos_on_grid(step, NPHI)
 
@@ -223,35 +221,59 @@
                 )
 
     lane = lax.broadcasted_iota(jnp.int32, (ROWS, LANES), 1)
+    blocks = 2 * per_tile
     imag_row = (lane // (depth * per_tile)) % 2
     sin_column = (lane // pairs) % 2
     part = (imag_row + sin_column) % 2
     code = ((lane // depth) % per_tile * 2 + part) * pairs + lane % pairs
     sign = jnp.where((imag_row == 0) & (sin_column == 1), -1.0, 1.0)
+    sign_column = jnp.where(sin_column == 1, -1.0, 1.0)
+
+    def totals(z, t, h):
+        beam = slab[z, pl.ds(wig_rows, beam_rows)].astype(F32)
+        at = t * tile_modes + h * ROWS
+        sky = [[sky_wide[r, c, pl.ds(at, ROWS)] for c in range(3)] for r in range(2)]
+        for p in range(planes):
+            re = im = 0.0
+            for c in range(3):
+                b0 = beam[c * planes + p : c * planes + p + 1]
+                b1 = beam[(3 + c) * planes + p : (3 + c) * planes + p + 1]
+                re = re + (sky[0][c] * b0 - sky[1][c] * b1)
+                im = im + (sky[0][c] * b1 + sky[1][c] * b0)
+            re = re.astype(BF16).astype(F32)
+            im = im.astype(BF16).astype(F32)
+            for g in range(cycles):
+                w = wide[g, pl.ds(at * planes + p, ROWS, stride=planes)]
+                for k, spectra in enumerate((re, im)):
+                    yield k, g * planes + p, jnp.sum(w * spectra, axis=1, keepdims=True)
 
     def profile(z):
-        beam = slab[z, pl.ds(wig_rows, beam_rows)].astype(F32)
         for t in range(tiles):
             packed = jnp.zeros((ROWS, LANES), F32)
             for h in range(per_tile):
-                at = t * tile_modes + h * ROWS
-                sky = [[sky_wide[r, c, pl.ds(at, ROWS)] for c in range(3)] for r in range(2)]
-                for p in range(planes):
-                    re = im = 0.0
-                    for c in range(3):
-                        b0 = beam[c * planes + p : c * planes + p + 1]
-                        b1 = beam[(3 + c) * planes + p : (3 + c) * planes + p + 1]
-                        re = re + (sky[0][c] * b0 - sky[1][c] * b1)
-                        im = im + (sky[0][c] * b1 + sky[1][c] * b0)
-                    re = re.astype(BF16).astype(F32)
-                    im = im.astype(BF16).astype(F32)
-                    for g in range(cycles):
-                        w = wide[g, pl.ds(at * planes + p, ROWS, stride=planes)]
-                        for k, spectra in enumerate((re, im)):
-                            total = jnp.sum(w * spectra, axis=1, keepdims=True)
-                            where = (h * 2 + k) * pairs + g * planes + p
-                            packed = jnp.where(code == where, total, packed)
+                for k, i, total in totals(z, t, h):
+                    packed = jnp.where(code == (h * 2 + k) * pairs + i, total, packed)
             cube_all[z, t] = packed * sign
+
+    def profile_here(z):
+        inner = lane - z * depth
+        inside = lane // depth == z
+        for t in range(tiles):
+            for h in range(per_tile):
+                real = imag = jnp.zeros((ROWS, LANES), F32)
+                for k, i, total in totals(z, t, h):
+                    cos_place, sin_place = inner == i, inner == pairs + i
+                    real = jnp.where(sin_place if k else cos_place, total, real)
+                    imag = jnp.where(cos_place if k else sin_place, total, imag)
+                left[t, h] = jnp.where(inside, real * sign_column, left[t, h])
+                left[t, per_tile + h] = jnp.where(inside, imag, left[t, per_tile + h])
+
+    def place(z):
+        inside = lane // depth == z
+        for t in range(tiles):
+            for q in range(blocks):
+                moved = pltpu.roll(cube_all[z, t], (z - q) % n_bm * depth, 1)
+                left[t, q] = jnp.where(inside, moved, left[t, q])
 
     profile(bm)
 
@@ -268,30 +290,30 @@
         def _():
             cube_to(z).start()
 
+    left[...] = jnp.zeros_like(left)
     for z in range(n_bm):
-        @pl.when(by_cube(z, bm))
-        def _():
-            landing(cube_all, z).wait_recv()
-        if pushes and z > 0:
+        @pl.when(bm == z)
+        def _():
+            place(z)
+
+    if pushes:
+        for z in range(1, n_bm):
             @pl.when(pushed(even, n_bm, z, bm))
             def _():
                 landing(slab, z).wait_recv()
                 widen(z)
-                profile(z)
-
-    blocks = []
-    for t in range(tiles):
-        parts = [cube_all[s, t] for s in range(n_bm)]
-        for q in range(2 * per_tile):
-            blocks.append(
-                jnp.concatenate([x[:, q * depth : (q + 1) * depth] for x in parts], axis=1)
-            )
-    left = jnp.concatenate(blocks, axis=0)
-    high = left.astype(BF16)
-    low = (left - high.astype(F32)).astype(BF16)
-    both = jnp.concatenate(
-        [jnp.concatenate([high, high], axis=1), jnp.concatenate([low, low], axis=1)], axis=0
-    )
+                profile_here(z)
+
+    for z in range(n_bm):
+        @pl.when(by_cube(z, bm))
+        def _():
+            landing(cube_all, z).wait_recv()
+            place(z)
+
+    wave = left[...].reshape(m_rows, k_rows)
+    high = wave.astype(BF16)
+    low = (wave - high.astype(F32)).astype(BF16)
+    both = jnp.concatenate([high, low], axis=0)
     y = jnp.dot(both, feat[...], preferred_element_type=F32)
     z = (y[:m_rows] + y[m_rows:]) * phase[...]
     total = jnp.sum(z, axis=0, keepdims=True)
@@ -334,9 +356,10 @@
             pltpu.VMEM((3, dets, samples), jnp.int32),
             pltpu.VMEM((2, 3, modes, band), F32),
             pltpu.VMEM((cycles, modes * planes, band), F32),
-            pltpu.VMEM((2 * n_bm * depth, ROWS * span), BF16),
+            pltpu.VMEM((n_bm * depth, ROWS * span), BF16),
             pltpu.VMEM((2 * modes, ROWS * span), F32),
             pltpu.VMEM((n_bm, tiles, ROWS, LANES), F32),
+            pltpu.VMEM((tiles, LANES // depth, ROWS, LANES), F32),
             pltpu.SemaphoreType.DMA((3,)),
             pltpu.SemaphoreType.DMA((2,)),
             pltpu.SemaphoreType.DMA((n_bm,)),

time: 10.7 us -> 10.6 us (level)
  Pallas kernels: 9.94 us -> 9.78 us
    pallas_call x1, Pallas kernels: 9.94 us -> 9.78 us  [on_device(): pl.pallas_call(functools.partial(kernel, n_det, n_bm, cycles, pushes), ou...]
where the time goes in v2:
time: 10.6 us; the launch traced here: 10.4 us
  Pallas kernels  9.78 us (92%)
  local copies, waits for them, and re-layouts  0.6 us (6%)
    pallas_call x1, Pallas kernels, on_device(): pl.pallas_call(functools.partial(kernel, n_det, n_bm, cycles, pushes), ou...  9.78 us
    unnamed x1, local copies, waits for them, and re-layouts  0.6 us

profile of v2, /device:TPU:1, one launch (start us, length us, event | category | flops | bytes accessed | tf_op | source)
XLA Modules:
  0.0 10.4 jit_solution(10621559170745488490)
XLA Ops:
  0.0 9.8 %shard_map.64 = f32[16,64]{1,0:T(8,128)S(1)} custom-call(bf16[2,3,2,128]{3,2,1,0:T(2,128)(2,1)} %sky_hbm.1, bf16[24,128]{1,0:T(8,128)(2,1)} %bitcast.3, bf16[256,128]{1,0:T(8,128)(2,1)} %bitcast.2, s32[16,256]{1,0:T(8,128)} %theta_hbm.1, s32[16,256]{1,0:T(8,128)} %phi_hbm.1, s32[16,256]{1,0:T(8,128)} %psi_hbm.1), custom_call_target="tpu_custom_call" | custom-call | tf_op jit(solution)/shard_map/pallas_call | solution.py:348
  9.8 0.6 %copy.8 = f32[16,64]{1,0:T(8,128)} copy(f32[16,64]{1,0:T(8,128)S(1)} %shard_map.64) | data formatting | bytes 8192

commit v3 on v2

--- a/solution.py
+++ b/solution.py
@@ -45,14 +45,14 @@
     return jnp.concatenate([values[j * ROWS : (j + 1) * ROWS] for j in range(groups)], axis=1)
 
 
-def pushed(even, n_bm, source, target):
-    return (even & (source > target) & (target == 0)) | (source - target >= n_bm - 1)
+def pushed(even, source, target):
+    return (source - target >= 2) | (even & (source > target) & (target == 0))
 
 
 def kernel(
-    n_det, n_bm, cycles, pushes,
+    n_det, n_bm, modes, pushes,
     sky_hbm, beam_hbm, wig_hbm, theta_hbm, phi_hbm, psi_hbm, out_ref,
-    sky_all, slab, index, sky_wide, wide, feat, phase, cube_all, left,
+    sky_all, slab, index, sky_wide, wide, feat, phase, cube_all, early, left,
     local_sem, sky_sem, col_send, col_recv, ok, hello,
 ):
     det = lax.axis_index("det")
@@ -62,13 +62,14 @@
     buddy = det + 1 - 2 * (det % 2)
     n_pairs = n_det // 2
 
-    rows, band = slab.shape[1:]
-    beam_rows = beam_hbm.shape[0]
-    wig_rows = rows - beam_rows
-    planes = beam_rows // 6
-    flat = wig_rows // cycles
-    modes = flat // planes
+    cycles, units, _, band = wig_hbm.shape
+    beam_units = beam_hbm.shape[0]
+    planes = beam_units * ROWS // 6
     owned = sky_all.shape[3]
+    chunks = n_pairs if pushes else 1
+    part_units = units // chunks
+    chunk_units = cycles * part_units
+    wig_units = cycles * units
     pairs = cycles * planes
     depth = 2 * pairs
     per_tile = LANES // (2 * depth)
@@ -79,13 +80,23 @@
     groups = dets // ROWS
 
     pltpu.make_async_copy(sky_hbm, sky_all.at[det], local_sem.at[0]).start()
-    for g in range(cycles):
-        part = pl.ds(g * flat, flat)
-        pltpu.make_async_copy(wig_hbm.at[part], slab.at[bm, part], local_sem.at[1]).start()
-    pltpu.make_async_copy(beam_hbm, slab.at[bm, pl.ds(wig_rows, beam_rows)], local_sem.at[1]).start()
-    pltpu.make_async_copy(theta_hbm, index.at[0], local_sem.at[2]).start()
-    pltpu.make_async_copy(phi_hbm, index.at[1], local_sem.at[2]).start()
-    pltpu.make_async_copy(psi_hbm, index.at[2], local_sem.at[2]).start()
+
+    def place_of(k):
+        return partner(pair, k, n_pairs) if pushes else 0
+
+    def fetch(k):
+        pltpu.make_async_copy(
+            wig_hbm.at[:, pl.ds(place_of(k) * part_units, part_units)],
+            slab.at[bm, pl.ds(k * chunk_units, chunk_units)].reshape(cycles, part_units, ROWS, band),
+            local_sem.at[2 + k],
+        ).start()
+
+    for k in range(1, chunks):
+        fetch(k)
+    pltpu.make_async_copy(
+        beam_hbm, slab.at[bm, pl.ds(wig_units, beam_units)], local_sem.at[1 + chunks]
+    ).start()
+    fetch(0)
 
     barrier = pltpu.get_barrier_semaphore()
 
@@ -99,10 +110,25 @@
             greet(barrier, 2 * pair + 1, z)
     for k in range(1, n_pairs):
         greet(barrier, 2 * ((pair + k) % n_pairs), bm)
-
-    def push_to(z):
+    pltpu.make_async_copy(theta_hbm, index.at[0], local_sem.at[1]).start()
+    pltpu.make_async_copy(phi_hbm, index.at[1], local_sem.at[1]).start()
+    pltpu.make_async_copy(psi_hbm, index.at[2], local_sem.at[1]).start()
+
+    def units_of(first, stop):
+        end = wig_units + beam_units if stop == chunks else stop * chunk_units
+        return pl.ds(first * chunk_units, end - first * chunk_units)
+
+    def push_to(z, first=1, stop=chunks):
+        part = slab.at[bm, units_of(first, stop)]
         return pltpu.make_async_remote_copy(
-            src_ref=slab.at[bm], dst_ref=slab.at[bm],
+            src_ref=part, dst_ref=part,
+            send_sem=col_send.at[z], recv_sem=col_recv.at[bm],
+            device_id=(det, z), device_id_type=MESH,
+        )
+
+    def early_to(z):
+        return pltpu.make_async_remote_copy(
+            src_ref=early.at[bm], dst_ref=early.at[bm],
             send_sem=col_send.at[z], recv_sem=col_recv.at[bm],
             device_id=(det, z), device_id_type=MESH,
         )
@@ -116,16 +142,31 @@
 
     def landing(buffer, z):
         return pltpu.make_async_remote_copy(
-            src_ref=buffer.at[z], dst_ref=buffer.at[z],
+            src_ref=buffer, dst_ref=buffer,
             send_sem=col_send.at[z], recv_sem=col_recv.at[z],
             device_id=(det, z), device_id_type=MESH,
         )
+
+    early_units = ROWS * LANES * 4 // (ROWS * band * 2)
+    moved = slab.at[bm, pl.ds(0, wig_units + beam_units - chunk_units + early_units)]
 
     @pl.when(jnp.logical_not(even))
     def _():
         pl.semaphore_wait(barrier, 1 + 2 * bm)
         greet(ok, buddy, bm)
 
+    @pl.when(even)
+    def _():
+        pl.semaphore_wait(ok, 1)
+
+    pltpu.make_async_copy(sky_hbm, sky_all.at[det], local_sem.at[0]).wait()
+    to_buddy = pltpu.make_async_remote_copy(
+        src_ref=sky_all.at[det], dst_ref=sky_all.at[det],
+        send_sem=sky_sem.at[2], recv_sem=sky_sem.at[3],
+        device_id=(buddy, bm), device_id_type=MESH,
+    )
+    to_buddy.start()
+
     def share_sky():
         @pl.when(even)
         def _():
@@ -136,29 +177,81 @@
         def _():
             pl.semaphore_wait(ok, 1)
 
-        pltpu.make_async_copy(sky_hbm, sky_all.at[det], local_sem.at[0]).wait()
-        for flip in range(n_det - 1, 0, -1):
+        for flip in range(n_det - 1, 1, -1):
             pltpu.make_async_remote_copy(
                 src_ref=sky_all.at[det], dst_ref=sky_all.at[det],
                 send_sem=sky_sem.at[0], recv_sem=sky_sem.at[1],
                 device_id=(partner(det, flip, n_det), bm), device_id_type=MESH,
             ).start()
 
+    lane = lax.broadcasted_iota(jnp.int32, (ROWS, LANES), 1)
+    blocks = 2 * per_tile
+    imag_row = (lane // (depth * per_tile)) % 2
+    sin_column = (lane // pairs) % 2
+    part = (imag_row + sin_column) % 2
+    code = ((lane // depth) % per_tile * 2 + part) * pairs + lane % pairs
+    sign = jnp.where((imag_row == 0) & (sin_column == 1), -1.0, 1.0)
+    sign_column = jnp.where(sin_column == 1, -1.0, 1.0)
+
+    def widen(z, first):
+        for k in range(first, chunks):
+            rows = pl.ds(pl.multiple_of(place_of(k) * part_units * ROWS, ROWS), part_units * ROWS)
+            for g in range(cycles):
+                block = slab[z, pl.ds(k * chunk_units + g * part_units, part_units)]
+                wide[g, rows] = block.astype(F32).reshape(part_units * ROWS, band)
+
+    def totals(z, sky, at):
+        beam = slab[z, pl.ds(wig_units, beam_units)].astype(F32).reshape(beam_units * ROWS, band)
+        for p in range(planes):
+            re = im = 0.0
+            for c in range(3):
+                b0 = beam[c * planes + p : c * planes + p + 1]
+                b1 = beam[(3 + c) * planes + p : (3 + c) * planes + p + 1]
+                re = re + (sky[0][c] * b0 - sky[1][c] * b1)
+                im = im + (sky[0][c] * b1 + sky[1][c] * b0)
+            re = re.astype(BF16).astype(F32)
+            im = im.astype(BF16).astype(F32)
+            for g in range(cycles):
+                w = wide[g, pl.ds(at * planes + p, ROWS, stride=planes)]
+                for k, spectra in enumerate((re, im)):
+                    yield k, g * planes + p, jnp.sum(w * spectra, axis=1, keepdims=True)
+
+    shared = 2 * owned
+    own_group = pair * shared // ROWS
+
+    def send_early():
+        to_buddy.wait_recv()
+        near = [
+            [
+                sky_all[pl.ds(2 * pair, 2), r, c].astype(F32).reshape(shared, band)
+                for c in range(3)
+            ]
+            for r in range(2)
+        ]
+        sky = [[jnp.concatenate([x] * (ROWS // shared), axis=0) for x in y] for y in near]
+        packed = jnp.zeros((ROWS, LANES), F32)
+        for k, i, total in totals(bm, sky, pl.multiple_of(own_group * ROWS, ROWS)):
+            packed = jnp.where(part * pairs + lane % pairs == k * pairs + i, total, packed)
+        early[bm] = packed * sign
+        early_to(0).start()
+
     def share_slab():
-        @pl.when(even)
-        def _():
-            pl.semaphore_wait(ok, 1)
-
+        for k in [*range(1, chunks), 0]:
+            part = slab.at[bm, units_of(k, k + 1)]
+            pltpu.make_async_copy(part, part, local_sem.at[2 + k]).wait()
+            if pushes and k:
+                @pl.when(pushed(even, bm, 0))
+                def _():
+                    push_to(0, k, k + 1).start()
         for z in range(n_bm - 1):
             @pl.when(bm > z)
             def _():
                 greet(hello, det, z)
-        pltpu.make_async_copy(slab.at[bm], slab.at[bm], local_sem.at[1]).wait()
+        widen(bm, 0)
         if pushes:
-            for z in range(n_bm - 1):
-                @pl.when(pushed(even, n_bm, bm, z))
-                def _():
-                    push_to(z).start()
+            @pl.when(pushed(even, bm, 0))
+            def _():
+                send_early()
 
     last = pair == n_pairs - 1
 
@@ -172,17 +265,23 @@
     def _():
         share_sky()
 
-    others = sky_all.at[pl.ds(0, n_det - 1)]
+    def share_inner(now):
+        for z in range(1, n_bm - 1):
+            @pl.when(now & pushed(even, bm, z))
+            def _():
+                push_to(z).start()
+                early_to(z).start()
+
+    if pushes:
+        share_inner(pair == 0)
+
+    others = sky_all.at[pl.ds(0, n_det - 2)]
     skies = pltpu.make_async_remote_copy(
         src_ref=others, dst_ref=others,
         send_sem=sky_sem.at[0], recv_sem=sky_sem.at[1],
         device_id=(buddy, bm), device_id_type=MESH,
     )
-    pltpu.make_async_copy(index, index, local_sem.at[2]).wait()
-
-    def widen(z):
-        for g in range(cycles):
-            wide[g] = slab[z, pl.ds(g * flat, flat)].astype(F32)
+    pltpu.make_async_copy(index, index, local_sem.at[1]).wait()
 
     def mine(values):
         own = values[:, :width]
@@ -209,7 +308,14 @@
         step = (mode * phi[j : j + 1] + mquarter) & (NPHI - 1)
         phase[:, at] = cos_on_grid(step, NPHI)
 
-    widen(bm)
+    if pushes:
+        share_inner(pair != 0)
+
+        @pl.when(jnp.logical_not(pushed(even, bm, 0)))
+        def _():
+            to_buddy.wait_recv()
+    else:
+        to_buddy.wait_recv()
     skies.wait_recv()
 
     slots = tile_modes // owned
@@ -220,38 +326,16 @@
                     sky_all[t * slots : (t + 1) * slots, r, c].astype(F32).reshape(tile_modes, band)
                 )
 
-    lane = lax.broadcasted_iota(jnp.int32, (ROWS, LANES), 1)
-    blocks = 2 * per_tile
-    imag_row = (lane // (depth * per_tile)) % 2
-    sin_column = (lane // pairs) % 2
-    part = (imag_row + sin_column) % 2
-    code = ((lane // depth) % per_tile * 2 + part) * pairs + lane % pairs
-    sign = jnp.where((imag_row == 0) & (sin_column == 1), -1.0, 1.0)
-    sign_column = jnp.where(sin_column == 1, -1.0, 1.0)
-
-    def totals(z, t, h):
-        beam = slab[z, pl.ds(wig_rows, beam_rows)].astype(F32)
+    def tile_totals(z, t, h):
         at = t * tile_modes + h * ROWS
         sky = [[sky_wide[r, c, pl.ds(at, ROWS)] for c in range(3)] for r in range(2)]
-        for p in range(planes):
-            re = im = 0.0
-            for c in range(3):
-                b0 = beam[c * planes + p : c * planes + p + 1]
-                b1 = beam[(3 + c) * planes + p : (3 + c) * planes + p + 1]
-                re = re + (sky[0][c] * b0 - sky[1][c] * b1)
-                im = im + (sky[0][c] * b1 + sky[1][c] * b0)
-            re = re.astype(BF16).astype(F32)
-            im = im.astype(BF16).astype(F32)
-            for g in range(cycles):
-                w = wide[g, pl.ds(at * planes + p, ROWS, stride=planes)]
-                for k, spectra in enumerate((re, im)):
-                    yield k, g * planes + p, jnp.sum(w * spectra, axis=1, keepdims=True)
+        return totals(z, sky, at)
 
     def profile(z):
         for t in range(tiles):
             packed = jnp.zeros((ROWS, LANES), F32)
             for h in range(per_tile):
-                for k, i, total in totals(z, t, h):
+                for k, i, total in tile_totals(z, t, h):
                     packed = jnp.where(code == (h * 2 + k) * pairs + i, total, packed)
             cube_all[z, t] = packed * sign
 
@@ -261,12 +345,17 @@
         for t in range(tiles):
             for h in range(per_tile):
                 real = imag = jnp.zeros((ROWS, LANES), F32)
-                for k, i, total in totals(z, t, h):
+                for k, i, total in tile_totals(z, t, h):
                     cos_place, sin_place = inner == i, inner == pairs + i
                     real = jnp.where(sin_place if k else cos_place, total, real)
                     imag = jnp.where(cos_place if k else sin_place, total, imag)
                 left[t, h] = jnp.where(inside, real * sign_column, left[t, h])
                 left[t, per_tile + h] = jnp.where(inside, imag, left[t, per_tile + h])
+        row = lax.broadcasted_iota(jnp.int32, (ROWS, LANES), 0)
+        known = inside & (row // shared == pair % (ROWS // shared))
+        for q in range(blocks):
+            ready = pltpu.roll(early[z], (z - q) % n_bm * depth, 1)
+            left[0, q] = jnp.where(known & (own_group == q % per_tile), ready, left[0, q])
 
     def place(z):
         inside = lane // depth == z
@@ -283,7 +372,7 @@
 
     def by_cube(source, target):
         apart = source != target
-        return apart & jnp.logical_not(pushed(even, n_bm, source, target)) if pushes else apart
+        return apart & jnp.logical_not(pushed(even, source, target)) if pushes else apart
 
     for z in range(n_bm - 1, -1, -1):
         @pl.when(by_cube(bm, z))
@@ -297,17 +386,17 @@
             place(z)
 
     if pushes:
-        for z in range(1, n_bm):
-            @pl.when(pushed(even, n_bm, z, bm))
+        for z in range(n_bm - 1, 0, -1):
+            @pl.when(pushed(even, z, bm))
             def _():
-                landing(slab, z).wait_recv()
-                widen(z)
+                landing(moved, z).wait_recv()
+                widen(z, 1)
                 profile_here(z)
 
     for z in range(n_bm):
         @pl.when(by_cube(z, bm))
         def _():
-            landing(cube_all, z).wait_recv()
+            landing(cube_all.at[z], z).wait_recv()
             place(z)
 
     wave = left[...].reshape(m_rows, k_rows)
@@ -323,14 +412,15 @@
             out_ref[pl.ds(i * ROWS + j, 1), :] = total[:, at : at + width]
 
     skies.wait_send()
+    to_buddy.wait_send()
     for z in range(n_bm):
         @pl.when(by_cube(bm, z))
         def _():
             cube_to(z).wait_send()
         if pushes and z < n_bm - 1:
-            @pl.when(pushed(even, n_bm, bm, z))
+            @pl.when(pushed(even, bm, z))
             def _():
-                push_to(z).wait_send()
+                landing(moved, z).wait_send()
 
 
 def on_device(sky_alm, beam_blm, wigner, theta_index, phi_index, psi_index):
@@ -342,26 +432,29 @@
     depth = 2 * cycles * planes
     tiles = modes * 2 * depth // (ROWS * LANES)
     beam_rows = 6 * planes
-    wig_rows = cycles * modes * planes
-    pushes = 2 * wig_rows * band <= PUSH_BYTES
+    units = modes * planes // ROWS
+    wig_units = cycles * units
+    beam_units = beam_rows // ROWS
+    pushes = tiles == 1 and 2 * wig_units * ROWS * band <= PUSH_BYTES
     any_space = pl.BlockSpec(memory_space=pl.ANY)
     return pl.pallas_call(
-        functools.partial(kernel, n_det, n_bm, cycles, pushes),
+        functools.partial(kernel, n_det, n_bm, modes, pushes),
         out_shape=pltpu.VMEM((dets, width), F32),
         in_specs=[any_space] * 6,
         out_specs=pl.BlockSpec(memory_space=pltpu.VMEM),
         scratch_shapes=[
             pltpu.VMEM((n_det, *sky_alm.shape), BF16),
-            pltpu.VMEM((n_bm, wig_rows + beam_rows, band), BF16),
+            pltpu.VMEM((n_bm, wig_units + beam_units, ROWS, band), BF16),
             pltpu.VMEM((3, dets, samples), jnp.int32),
             pltpu.VMEM((2, 3, modes, band), F32),
             pltpu.VMEM((cycles, modes * planes, band), F32),
             pltpu.VMEM((n_bm * depth, ROWS * span), BF16),
             pltpu.VMEM((2 * modes, ROWS * span), F32),
             pltpu.VMEM((n_bm, tiles, ROWS, LANES), F32),
+            pltpu.VMEM((n_bm, ROWS, LANES), F32),
             pltpu.VMEM((tiles, LANES // depth, ROWS, LANES), F32),
-            pltpu.SemaphoreType.DMA((3,)),
-            pltpu.SemaphoreType.DMA((2,)),
+            pltpu.SemaphoreType.DMA((2 + (n_det // 2 if pushes else 1),)),
+            pltpu.SemaphoreType.DMA((4,)),
             pltpu.SemaphoreType.DMA((n_bm,)),
             pltpu.SemaphoreType.DMA((n_bm,)),
             pltpu.SemaphoreType.REGULAR,
@@ -370,8 +463,8 @@
         compiler_params=pltpu.CompilerParams(collective_id=0, has_side_effects=True),
     )(
         sky_alm,
-        beam_blm.reshape(beam_rows, band),
-        wigner.reshape(wig_rows, band),
+        beam_blm.reshape(beam_units, ROWS, band),
+        wigner.reshape(cycles, units, ROWS, band),
         theta_index,
         phi_index,
         psi_index,

time: 10.6 us -> 9.9 us (0.934)
  the two profiles are of different devices: /device:TPU:1 before, /device:TPU:0 now
where the time goes in v3:
time: 9.9 us; the launch traced here: 9.73 us
  Pallas kernels  9.12 us (92%)
  local copies, waits for them, and re-layouts  0.6 us (6%)
    pallas_call x1, Pallas kernels, on_device(): pl.pallas_call(functools.partial(kernel, n_det, n_bm, modes, pushes), out...  9.12 us
    unnamed x1, local copies, waits for them, and re-layouts  0.6 us

profile of v3, /device:TPU:0, one launch (start us, length us, event | category | flops | bytes accessed | tf_op | source)
XLA Modules:
  0.0 9.7 jit_solution(11498567772080909200)
XLA Ops:
  0.0 9.1 %shard_map.64 = f32[16,64]{1,0:T(8,128)S(1)} custom-call(bf16[2,3,2,128]{3,2,1,0:T(2,128)(2,1)} %sky_hbm.1, bf16[3,8,128]{2,1,0:T(8,128)(2,1)} %bitcast.3, bf16[4,8,8,128]{3,2,1,0:T(8,128)(2,1)} %bitcast.2, s32[16,256]{1,0:T(8,128)} %theta_hbm.1, s32[16,256]{1,0:T(8,128)} %phi_hbm.1, s32[16,256]{1,0:T(8,128)} %psi_hbm.1), custom_call_target="tpu_custom_call" | custom-call | tf_op jit(solution)/shard_map/pallas_call | solution.py:440
  9.1 0.6 %copy.8 = f32[16,64]{1,0:T(8,128)} copy(f32[16,64]{1,0:T(8,128)S(1)} %shard_map.64) | data formatting | bytes 8192

commit v4 on v3

--- a/solution.py
+++ b/solution.py
@@ -45,8 +45,10 @@
     return jnp.concatenate([values[j * ROWS : (j + 1) * ROWS] for j in range(groups)], axis=1)
 
 
-def pushed(even, source, target):
-    return (source - target >= 2) | (even & (source > target) & (target == 0))
+def pushed(role, source, target):
+    even, inner = role
+    near = even & (source > target) & (target == 0)
+    return near | ((source - target >= 2) & (inner | (target == 0)))
 
 
 def kernel(
@@ -61,6 +63,7 @@
     pair = det // 2
     buddy = det + 1 - 2 * (det % 2)
     n_pairs = n_det // 2
+    role = even, even | (pair != n_pairs - 1)
 
     cycles, units, _, band = wig_hbm.shape
     beam_units = beam_hbm.shape[0]
@@ -235,12 +238,14 @@
         early[bm] = packed * sign
         early_to(0).start()
 
+    yields = jnp.logical_not(even) & (pair == 0) & (bm == n_bm - 1)
+
     def share_slab():
         for k in [*range(1, chunks), 0]:
             part = slab.at[bm, units_of(k, k + 1)]
             pltpu.make_async_copy(part, part, local_sem.at[2 + k]).wait()
             if pushes and k:
-                @pl.when(pushed(even, bm, 0))
+                @pl.when(jnp.logical_not(yields) & pushed(role, bm, 0))
                 def _():
                     push_to(0, k, k + 1).start()
         for z in range(n_bm - 1):
@@ -249,9 +254,13 @@
                 greet(hello, det, z)
         widen(bm, 0)
         if pushes:
-            @pl.when(pushed(even, bm, 0))
+            @pl.when(pushed(role, bm, 0))
             def _():
                 send_early()
+
+            @pl.when(yields & pushed(role, bm, 0))
+            def _():
+                push_to(0).start()
 
     last = pair == n_pairs - 1
 
@@ -267,13 +276,13 @@
 
     def share_inner(now):
         for z in range(1, n_bm - 1):
-            @pl.when(now & pushed(even, bm, z))
+            @pl.when(now & pushed(role, bm, z))
             def _():
                 push_to(z).start()
                 early_to(z).start()
 
     if pushes:
-        share_inner(pair == 0)
+        share_inner((pair == 0) | jnp.logical_not(even))
 
     others = sky_all.at[pl.ds(0, n_det - 2)]
     skies = pltpu.make_async_remote_copy(
@@ -309,9 +318,9 @@
         phase[:, at] = cos_on_grid(step, NPHI)
 
     if pushes:
-        share_inner(pair != 0)
-
-        @pl.when(jnp.logical_not(pushed(even, bm, 0)))
+        share_inner((pair != 0) & even)
+
+        @pl.when(jnp.logical_not(pushed(role, bm, 0)))
         def _():
             to_buddy.wait_recv()
     else:
@@ -372,7 +381,7 @@
 
     def by_cube(source, target):
         apart = source != target
-        return apart & jnp.logical_not(pushed(even, source, target)) if pushes else apart
+        return apart & jnp.logical_not(pushed(role, source, target)) if pushes else apart
 
     for z in range(n_bm - 1, -1, -1):
         @pl.when(by_cube(bm, z))
@@ -386,8 +395,8 @@
             place(z)
 
     if pushes:
-        for z in range(n_bm - 1, 0, -1):
-            @pl.when(pushed(even, z, bm))
+        for z in range(1, n_bm):
+            @pl.when(pushed(role, z, bm))
             def _():
                 landing(moved, z).wait_recv()
                 widen(z, 1)
@@ -418,7 +427,7 @@
         def _():
             cube_to(z).wait_send()
         if pushes and z < n_bm - 1:
-            @pl.when(pushed(even, bm, z))
+            @pl.when(pushed(role, bm, z))
             def _():
                 landing(moved, z).wait_send()
 

time: 9.9 us -> 9.52 us (0.962)
  the two profiles are of different devices: /device:TPU:0 before, /device:TPU:1 now
where the time goes in v4:
time: 9.52 us; the launch traced here: 9.35 us
  Pallas kernels  8.74 us (92%)
  local copies, waits for them, and re-layouts  0.6 us (6%)
    pallas_call x1, Pallas kernels, on_device(): pl.pallas_call(functools.partial(kernel, n_det, n_bm, modes, pushes), out...  8.74 us
    unnamed x1, local copies, waits for them, and re-layouts  0.6 us

profile of v4, /device:TPU:1, one launch (start us, length us, event | category | flops | bytes accessed | tf_op | source)
XLA Modules:
  0.0 9.3 jit_solution(6470408547173982407)
XLA Ops:
  0.0 8.7 %shard_map.64 = f32[16,64]{1,0:T(8,128)S(1)} custom-call(bf16[2,3,2,128]{3,2,1,0:T(2,128)(2,1)} %sky_hbm.1, bf16[3,8,128]{2,1,0:T(8,128)(2,1)} %bitcast.3, bf16[4,8,8,128]{3,2,1,0:T(8,128)(2,1)} %bitcast.2, s32[16,256]{1,0:T(8,128)} %theta_hbm.1, s32[16,256]{1,0:T(8,128)} %phi_hbm.1, s32[16,256]{1,0:T(8,128)} %psi_hbm.1), custom_call_target="tpu_custom_call" | custom-call | tf_op jit(solution)/shard_map/pallas_call | solution.py:449
  8.7 0.6 %copy.8 = f32[16,64]{1,0:T(8,128)} copy(f32[16,64]{1,0:T(8,128)S(1)} %shard_map.64) | data formatting | bytes 8192

commit v5 on v4

--- a/solution.py
+++ b/solution.py
@@ -45,17 +45,17 @@
     return jnp.concatenate([values[j * ROWS : (j + 1) * ROWS] for j in range(groups)], axis=1)
 
 
-def pushed(role, source, target):
+def pushed(role, n_bm, source, target):
     even, inner = role
-    near = even & (source > target) & (target == 0)
-    return near | ((source - target >= 2) & (inner | (target == 0)))
+    top = even & (source == n_bm - 1)
+    return (source > target) & ((target == 0) | top | (inner & (source - target >= 2)))
 
 
 def kernel(
     n_det, n_bm, modes, pushes,
     sky_hbm, beam_hbm, wig_hbm, theta_hbm, phi_hbm, psi_hbm, out_ref,
     sky_all, slab, index, sky_wide, wide, feat, phase, cube_all, early, left,
-    local_sem, sky_sem, col_send, col_recv, ok, hello,
+    sky_sem, col_send, col_recv, ok, hello,
 ):
     det = lax.axis_index("det")
     bm = lax.axis_index("bm")
@@ -82,7 +82,8 @@
     width = samples // n_bm
     groups = dets // ROWS
 
-    pltpu.make_async_copy(sky_hbm, sky_all.at[det], local_sem.at[0]).start()
+    load = pltpu.make_async_copy(sky_hbm, sky_all.at[det], col_recv.at[bm])
+    load.start()
 
     def place_of(k):
         return partner(pair, k, n_pairs) if pushes else 0
@@ -91,13 +92,13 @@
         pltpu.make_async_copy(
             wig_hbm.at[:, pl.ds(place_of(k) * part_units, part_units)],
             slab.at[bm, pl.ds(k * chunk_units, chunk_units)].reshape(cycles, part_units, ROWS, band),
-            local_sem.at[2 + k],
+            col_send.at[bm],
         ).start()
 
     for k in range(1, chunks):
         fetch(k)
     pltpu.make_async_copy(
-        beam_hbm, slab.at[bm, pl.ds(wig_units, beam_units)], local_sem.at[1 + chunks]
+        beam_hbm, slab.at[bm, pl.ds(wig_units, beam_units)], col_send.at[bm]
     ).start()
     fetch(0)
 
@@ -113,18 +114,12 @@
             greet(barrier, 2 * pair + 1, z)
     for k in range(1, n_pairs):
         greet(barrier, 2 * ((pair + k) % n_pairs), bm)
-    pltpu.make_async_copy(theta_hbm, index.at[0], local_sem.at[1]).start()
-    pltpu.make_async_copy(phi_hbm, index.at[1], local_sem.at[1]).start()
-    pltpu.make_async_copy(psi_hbm, index.at[2], local_sem.at[1]).start()
-
-    def units_of(first, stop):
-        end = wig_units + beam_units if stop == chunks else stop * chunk_units
-        return pl.ds(first * chunk_units, end - first * chunk_units)
-
-    def push_to(z, first=1, stop=chunks):
-        part = slab.at[bm, units_of(first, stop)]
+
+    sent = pl.ds(chunk_units, wig_units + beam_units - chunk_units)
+
+    def push_to(z):
         return pltpu.make_async_remote_copy(
-            src_ref=part, dst_ref=part,
+            src_ref=slab.at[bm, sent], dst_ref=slab.at[bm, sent],
             send_sem=col_send.at[z], recv_sem=col_recv.at[bm],
             device_id=(det, z), device_id_type=MESH,
         )
@@ -162,13 +157,16 @@
     def _():
         pl.semaphore_wait(ok, 1)
 
-    pltpu.make_async_copy(sky_hbm, sky_all.at[det], local_sem.at[0]).wait()
+    load.wait()
     to_buddy = pltpu.make_async_remote_copy(
         src_ref=sky_all.at[det], dst_ref=sky_all.at[det],
-        send_sem=sky_sem.at[2], recv_sem=sky_sem.at[3],
+        send_sem=sky_sem.at[0], recv_sem=sky_sem.at[2],
         device_id=(buddy, bm), device_id_type=MESH,
     )
     to_buddy.start()
+    pltpu.make_async_copy(theta_hbm, index.at[0], col_recv.at[bm]).start()
+    pltpu.make_async_copy(phi_hbm, index.at[1], col_recv.at[bm]).start()
+    pltpu.make_async_copy(psi_hbm, index.at[2], col_recv.at[bm]).start()
 
     def share_sky():
         @pl.when(even)
@@ -241,24 +239,22 @@
     yields = jnp.logical_not(even) & (pair == 0) & (bm == n_bm - 1)
 
     def share_slab():
-        for k in [*range(1, chunks), 0]:
-            part = slab.at[bm, units_of(k, k + 1)]
-            pltpu.make_async_copy(part, part, local_sem.at[2 + k]).wait()
-            if pushes and k:
-                @pl.when(jnp.logical_not(yields) & pushed(role, bm, 0))
-                def _():
-                    push_to(0, k, k + 1).start()
+        pltpu.make_async_copy(slab.at[bm], slab.at[bm], col_send.at[bm]).wait()
+        if pushes:
+            @pl.when(jnp.logical_not(yields) & pushed(role, n_bm, bm, 0))
+            def _():
+                push_to(0).start()
         for z in range(n_bm - 1):
             @pl.when(bm > z)
             def _():
                 greet(hello, det, z)
         widen(bm, 0)
         if pushes:
-            @pl.when(pushed(role, bm, 0))
+            @pl.when(pushed(role, n_bm, bm, 0))
             def _():
                 send_early()
 
-            @pl.when(yields & pushed(role, bm, 0))
+            @pl.when(yields & pushed(role, n_bm, bm, 0))
             def _():
                 push_to(0).start()
 
@@ -276,7 +272,7 @@
 
     def share_inner(now):
         for z in range(1, n_bm - 1):
-            @pl.when(now & pushed(role, bm, z))
+            @pl.when(now & pushed(role, n_bm, bm, z))
             def _():
                 push_to(z).start()
                 early_to(z).start()
@@ -290,7 +286,7 @@
         send_sem=sky_sem.at[0], recv_sem=sky_sem.at[1],
         device_id=(buddy, bm), device_id_type=MESH,
     )
-    pltpu.make_async_copy(index, index, local_sem.at[1]).wait()
+    pltpu.make_async_copy(index, index, col_recv.at[bm]).wait()
 
     def mine(values):
         own = values[:, :width]
@@ -320,7 +316,7 @@
     if pushes:
         share_inner((pair != 0) & even)
 
-        @pl.when(jnp.logical_not(pushed(role, bm, 0)))
+        @pl.when(jnp.logical_not(pushed(role, n_bm, bm, 0)))
         def _():
             to_buddy.wait_recv()
     else:
@@ -381,7 +377,7 @@
 
     def by_cube(source, target):
         apart = source != target
-        return apart & jnp.logical_not(pushed(role, source, target)) if pushes else apart
+        return apart & jnp.logical_not(pushed(role, n_bm, source, target)) if pushes else apart
 
     for z in range(n_bm - 1, -1, -1):
         @pl.when(by_cube(bm, z))
@@ -396,7 +392,7 @@
 
     if pushes:
         for z in range(1, n_bm):
-            @pl.when(pushed(role, z, bm))
+            @pl.when(pushed(role, n_bm, z, bm))
             def _():
                 landing(moved, z).wait_recv()
                 widen(z, 1)
@@ -420,14 +416,19 @@
             at = j * span + i * width
             out_ref[pl.ds(i * ROWS + j, 1), :] = total[:, at : at + width]
 
-    skies.wait_send()
-    to_buddy.wait_send()
+    every = sky_all.at[pl.ds(0, n_det - 1)]
+    outbound = pltpu.make_async_remote_copy(
+        src_ref=every, dst_ref=every,
+        send_sem=sky_sem.at[0], recv_sem=sky_sem.at[1],
+        device_id=(buddy, bm), device_id_type=MESH,
+    )
+    outbound.wait_send()
     for z in range(n_bm):
         @pl.when(by_cube(bm, z))
         def _():
             cube_to(z).wait_send()
         if pushes and z < n_bm - 1:
-            @pl.when(pushed(role, bm, z))
+            @pl.when(pushed(role, n_bm, bm, z))
             def _():
                 landing(moved, z).wait_send()
 
@@ -462,8 +463,7 @@
             pltpu.VMEM((n_bm, tiles, ROWS, LANES), F32),
             pltpu.VMEM((n_bm, ROWS, LANES), F32),
             pltpu.VMEM((tiles, LANES // depth, ROWS, LANES), F32),
-            pltpu.SemaphoreType.DMA((2 + (n_det // 2 if pushes else 1),)),
-            pltpu.SemaphoreType.DMA((4,)),
+            pltpu.SemaphoreType.DMA((3,)),
             pltpu.SemaphoreType.DMA((n_bm,)),
             pltpu.SemaphoreType.DMA((n_bm,)),
             pltpu.SemaphoreType.REGULAR,

time: 9.52 us -> 9.47 us (level)
  the two profiles are of different devices: /device:TPU:1 before, /device:TPU:0 now
where the time goes in v5:
time: 9.47 us; the launch traced here: 9.29 us
  Pallas kernels  8.68 us (92%)
  local copies, waits for them, and re-layouts  0.6 us (6%)
    pallas_call x1, Pallas kernels, on_device(): pl.pallas_call(functools.partial(kernel, n_det, n_bm, modes, pushes), out...  8.68 us
    unnamed x1, local copies, waits for them, and re-layouts  0.6 us

profile of v5, /device:TPU:0, one launch (start us, length us, event | category | flops | bytes accessed | tf_op | source)
XLA Modules:
  0.0 9.3 jit_solution(10459840621618690273)
XLA Ops:
  0.0 8.7 %shard_map.64 = f32[16,64]{1,0:T(8,128)S(1)} custom-call(bf16[2,3,2,128]{3,2,1,0:T(2,128)(2,1)} %sky_hbm.1, bf16[3,8,128]{2,1,0:T(8,128)(2,1)} %bitcast.3, bf16[4,8,8,128]{3,2,1,0:T(8,128)(2,1)} %bitcast.2, s32[16,256]{1,0:T(8,128)} %theta_hbm.1, s32[16,256]{1,0:T(8,128)} %phi_hbm.1, s32[16,256]{1,0:T(8,128)} %psi_hbm.1), custom_call_target="tpu_custom_call" | custom-call | tf_op jit(solution)/shard_map/pallas_call | solution.py:450
  8.7 0.6 %copy.8 = f32[16,64]{1,0:T(8,128)} copy(f32[16,64]{1,0:T(8,128)S(1)} %shard_map.64) | data formatting | bytes 8192

commit v6 on v5

--- a/solution.py
+++ b/solution.py
@@ -82,25 +82,40 @@
     width = samples // n_bm
     groups = dets // ROWS
 
-    load = pltpu.make_async_copy(sky_hbm, sky_all.at[det], col_recv.at[bm])
-    load.start()
+    load = pltpu.make_async_copy(sky_hbm, sky_all.at[det], sky_sem.at[0])
 
     def place_of(k):
         return partner(pair, k, n_pairs) if pushes else 0
+
+    lead_sem = col_send.at[(bm + n_bm - 1) % n_bm]
 
     def fetch(k):
         pltpu.make_async_copy(
             wig_hbm.at[:, pl.ds(place_of(k) * part_units, part_units)],
             slab.at[bm, pl.ds(k * chunk_units, chunk_units)].reshape(cycles, part_units, ROWS, band),
-            col_send.at[bm],
+            lead_sem if k == 1 else col_send.at[bm],
         ).start()
 
-    for k in range(1, chunks):
-        fetch(k)
-    pltpu.make_async_copy(
-        beam_hbm, slab.at[bm, pl.ds(wig_units, beam_units)], col_send.at[bm]
-    ).start()
-    fetch(0)
+    def fetch_all():
+        for k in range(2, chunks):
+            fetch(k)
+        pltpu.make_async_copy(
+            beam_hbm, slab.at[bm, pl.ds(wig_units, beam_units)], col_send.at[bm]
+        ).start()
+        fetch(0)
+
+    last = pair == n_pairs - 1
+
+    @pl.when(jnp.logical_not(last))
+    def _():
+        if pushes:
+            fetch(1)
+        load.start()
+        fetch_all()
+
+    @pl.when(last)
+    def _():
+        load.start()
 
     barrier = pltpu.get_barrier_semaphore()
 
@@ -115,11 +130,19 @@
     for k in range(1, n_pairs):
         greet(barrier, 2 * ((pair + k) % n_pairs), bm)
 
-    sent = pl.ds(chunk_units, wig_units + beam_units - chunk_units)
-
-    def push_to(z):
+    @pl.when(last)
+    def _():
+        if pushes:
+            fetch(1)
+        fetch_all()
+
+    slab_units = wig_units + beam_units
+    sent_units = slab_units - chunk_units
+
+    def push_to(z, first=chunk_units, stop=slab_units):
+        part = slab.at[bm, pl.ds(first, stop - first)]
         return pltpu.make_async_remote_copy(
-            src_ref=slab.at[bm, sent], dst_ref=slab.at[bm, sent],
+            src_ref=part, dst_ref=part,
             send_sem=col_send.at[z], recv_sem=col_recv.at[bm],
             device_id=(det, z), device_id_type=MESH,
         )
@@ -146,7 +169,7 @@
         )
 
     early_units = ROWS * LANES * 4 // (ROWS * band * 2)
-    moved = slab.at[bm, pl.ds(0, wig_units + beam_units - chunk_units + early_units)]
+    moved = slab.at[bm, pl.ds(0, sent_units + early_units)]
 
     @pl.when(jnp.logical_not(even))
     def _():
@@ -156,6 +179,23 @@
     @pl.when(even)
     def _():
         pl.semaphore_wait(ok, 1)
+
+    if pushes:
+        yields = jnp.logical_not(even) & (pair == 0) & (bm == n_bm - 1)
+        at_once = jnp.logical_not(yields) & pushed(role, n_bm, bm, 0)
+
+    def share_lead():
+        part = slab.at[bm, pl.ds(chunk_units, chunk_units)]
+        pltpu.make_async_copy(part, part, lead_sem).wait()
+
+        @pl.when(at_once)
+        def _():
+            push_to(0, chunk_units, 2 * chunk_units).start()
+
+    if pushes:
+        @pl.when(jnp.logical_not(last))
+        def _():
+            share_lead()
 
     load.wait()
     to_buddy = pltpu.make_async_remote_copy(
@@ -236,14 +276,18 @@
         early[bm] = packed * sign
         early_to(0).start()
 
-    yields = jnp.logical_not(even) & (pair == 0) & (bm == n_bm - 1)
-
     def share_slab():
-        pltpu.make_async_copy(slab.at[bm], slab.at[bm], col_send.at[bm]).wait()
         if pushes:
-            @pl.when(jnp.logical_not(yields) & pushed(role, n_bm, bm, 0))
-            def _():
-                push_to(0).start()
+            @pl.when(last)
+            def _():
+                share_lead()
+
+        rest = slab.at[bm, pl.ds(0, slab_units - chunk_units if pushes else slab_units)]
+        pltpu.make_async_copy(rest, rest, col_send.at[bm]).wait()
+        if pushes:
+            @pl.when(at_once)
+            def _():
+                push_to(0, 2 * chunk_units).start()
         for z in range(n_bm - 1):
             @pl.when(bm > z)
             def _():
@@ -257,8 +301,6 @@
             @pl.when(yields & pushed(role, n_bm, bm, 0))
             def _():
                 push_to(0).start()
-
-    last = pair == n_pairs - 1
 
     @pl.when(last)
     def _():
@@ -390,31 +432,49 @@
         def _():
             place(z)
 
+    def take(z):
+        landing(moved, z).wait_recv()
+        widen(z, 1)
+        profile_here(z)
+
+    def finish():
+        wave = left[...].reshape(m_rows, k_rows)
+        high = wave.astype(BF16)
+        low = (wave - high.astype(F32)).astype(BF16)
+        both = jnp.concatenate([high, low], axis=0)
+        y = jnp.dot(both, feat[...], preferred_element_type=F32)
+        terms = (y[:m_rows] + y[m_rows:]) * phase[...]
+        total = jnp.sum(terms, axis=0, keepdims=True)
+        for j in range(ROWS):
+            for i in range(groups):
+                at = j * span + i * width
+                out_ref[pl.ds(i * ROWS + j, 1), :] = total[:, at : at + width]
+
+    def finish_mixed():
+        if pushes:
+            for z in range(1, n_bm):
+                @pl.when(pushed(role, n_bm, z, bm))
+                def _():
+                    take(z)
+        for z in range(n_bm):
+            @pl.when(by_cube(z, bm))
+            def _():
+                landing(cube_all.at[z], z).wait_recv()
+                place(z)
+        finish()
+
     if pushes:
-        for z in range(1, n_bm):
-            @pl.when(pushed(role, n_bm, z, bm))
-            def _():
-                landing(moved, z).wait_recv()
-                widen(z, 1)
-                profile_here(z)
-
-    for z in range(n_bm):
-        @pl.when(by_cube(z, bm))
-        def _():
-            landing(cube_all.at[z], z).wait_recv()
-            place(z)
-
-    wave = left[...].reshape(m_rows, k_rows)
-    high = wave.astype(BF16)
-    low = (wave - high.astype(F32)).astype(BF16)
-    both = jnp.concatenate([high, low], axis=0)
-    y = jnp.dot(both, feat[...], preferred_element_type=F32)
-    z = (y[:m_rows] + y[m_rows:]) * phase[...]
-    total = jnp.sum(z, axis=0, keepdims=True)
-    for j in range(ROWS):
-        for i in range(groups):
-            at = j * span + i * width
-            out_ref[pl.ds(i * ROWS + j, 1), :] = total[:, at : at + width]
+        @pl.when(bm == 0)
+        def _():
+            for z in range(1, n_bm):
+                take(z)
+            finish()
+
+        @pl.when(bm > 0)
+        def _():
+            finish_mixed()
+    else:
+        finish_mixed()
 
     every = sky_all.at[pl.ds(0, n_det - 1)]
     outbound = pltpu.make_async_remote_copy(

time: 9.47 us -> 9.37 us (0.989)
  no operation moved by 1% of the time
where the time goes in v6:
time: 9.37 us; the launch traced here: 9.2 us
  Pallas kernels  8.59 us (92%)
  local copies, waits for them, and re-layouts  0.6 us (6%)
    pallas_call x1, Pallas kernels, on_device(): pl.pallas_call(functools.partial(kernel, n_det, n_bm, modes, pushes), out...  8.59 us
    unnamed x1, local copies, waits for them, and re-layouts  0.6 us

profile of v6, /device:TPU:0, one launch (start us, length us, event | category | flops | bytes accessed | tf_op | source)
XLA Modules:
  0.0 9.2 jit_solution(14835507860038022220)
XLA Ops:
  0.0 8.6 %shard_map.64 = f32[16,64]{1,0:T(8,128)S(1)} custom-call(bf16[2,3,2,128]{3,2,1,0:T(2,128)(2,1)} %sky_hbm.1, bf16[3,8,128]{2,1,0:T(8,128)(2,1)} %bitcast.3, bf16[4,8,8,128]{3,2,1,0:T(8,128)(2,1)} %bitcast.2, s32[16,256]{1,0:T(8,128)} %theta_hbm.1, s32[16,256]{1,0:T(8,128)} %phi_hbm.1, s32[16,256]{1,0:T(8,128)} %psi_hbm.1), custom_call_target="tpu_custom_call" | custom-call | tf_op jit(solution)/shard_map/pallas_call | solution.py:510
  8.6 0.6 %copy.8 = f32[16,64]{1,0:T(8,128)} copy(f32[16,64]{1,0:T(8,128)S(1)} %shard_map.64) | data formatting | bytes 8192

commit v7 on v6

--- a/solution.py
+++ b/solution.py
@@ -106,16 +106,19 @@
 
     last = pair == n_pairs - 1
 
-    @pl.when(jnp.logical_not(last))
+    ahead = even & jnp.logical_not(last)
+
+    @pl.when(ahead)
     def _():
         if pushes:
             fetch(1)
         load.start()
         fetch_all()
 
-    @pl.when(last)
+    @pl.when(jnp.logical_not(ahead))
     def _():
         load.start()
+
 
     barrier = pltpu.get_barrier_semaphore()
 
@@ -130,7 +133,7 @@
     for k in range(1, n_pairs):
         greet(barrier, 2 * ((pair + k) % n_pairs), bm)
 
-    @pl.when(last)
+    @pl.when(jnp.logical_not(ahead))
     def _():
         if pushes:
             fetch(1)
@@ -193,7 +196,7 @@
             push_to(0, chunk_units, 2 * chunk_units).start()
 
     if pushes:
-        @pl.when(jnp.logical_not(last))
+        @pl.when(ahead)
         def _():
             share_lead()
 
@@ -278,7 +281,7 @@
 
     def share_slab():
         if pushes:
-            @pl.when(last)
+            @pl.when(jnp.logical_not(ahead))
             def _():
                 share_lead()
 

time: 9.37 us -> 9.36 us (level)
  no operation moved by 1% of the time
where the time goes in v7:
time: 9.36 us; the launch traced here: 9.19 us
  Pallas kernels  8.58 us (92%)
  local copies, waits for them, and re-layouts  0.6 us (6%)
    pallas_call x1, Pallas kernels, on_device(): pl.pallas_call(functools.partial(kernel, n_det, n_bm, modes, pushes), out...  8.58 us
    unnamed x1, local copies, waits for them, and re-layouts  0.6 us

profile of v7, /device:TPU:0, one launch (start us, length us, event | category | flops | bytes accessed | tf_op | source)
XLA Modules:
  0.0 9.2 jit_solution(11721442838738187715)
XLA Ops:
  0.0 8.6 %shard_map.64 = f32[16,64]{1,0:T(8,128)S(1)} custom-call(bf16[2,3,2,128]{3,2,1,0:T(2,128)(2,1)} %sky_hbm.1, bf16[3,8,128]{2,1,0:T(8,128)(2,1)} %bitcast.3, bf16[4,8,8,128]{3,2,1,0:T(8,128)(2,1)} %bitcast.2, s32[16,256]{1,0:T(8,128)} %theta_hbm.1, s32[16,256]{1,0:T(8,128)} %phi_hbm.1, s32[16,256]{1,0:T(8,128)} %psi_hbm.1), custom_call_target="tpu_custom_call" | custom-call | tf_op jit(solution)/shard_map/pallas_call | solution.py:513
  8.6 0.6 %copy.8 = f32[16,64]{1,0:T(8,128)} copy(f32[16,64]{1,0:T(8,128)S(1)} %shard_map.64) | data formatting | bytes 8192

commit v8 on v7

--- a/solution.py
+++ b/solution.py
@@ -237,8 +237,8 @@
     sign = jnp.where((imag_row == 0) & (sin_column == 1), -1.0, 1.0)
     sign_column = jnp.where(sin_column == 1, -1.0, 1.0)
 
-    def widen(z, first):
-        for k in range(first, chunks):
+    def widen(z, first, stop=chunks):
+        for k in range(first, stop):
             rows = pl.ds(pl.multiple_of(place_of(k) * part_units * ROWS, ROWS), part_units * ROWS)
             for g in range(cycles):
                 block = slab[z, pl.ds(k * chunk_units + g * part_units, part_units)]
@@ -279,6 +279,8 @@
         early[bm] = packed * sign
         early_to(0).start()
 
+    near_chunks = min(chunks, max(1, ROWS // (2 * sky_all.shape[3]))) if pushes else chunks
+
     def share_slab():
         if pushes:
             @pl.when(jnp.logical_not(ahead))
@@ -295,7 +297,7 @@
             @pl.when(bm > z)
             def _():
                 greet(hello, det, z)
-        widen(bm, 0)
+        widen(bm, 0, near_chunks)
         if pushes:
             @pl.when(pushed(role, n_bm, bm, 0))
             def _():
@@ -304,6 +306,8 @@
             @pl.when(yields & pushed(role, n_bm, bm, 0))
             def _():
                 push_to(0).start()
+
+        widen(bm, near_chunks)
 
     @pl.when(last)
     def _():

time: 9.36 us -> 9.36 us (level)
  no operation moved by 1% of the time
where the time goes in v8:
time: 9.36 us; the launch traced here: 9.19 us
  Pallas kernels  8.58 us (92%)
  local copies, waits for them, and re-layouts  0.6 us (6%)
    pallas_call x1, Pallas kernels, on_device(): pl.pallas_call(functools.partial(kernel, n_det, n_bm, modes, pushes), out...  8.58 us
    unnamed x1, local copies, waits for them, and re-layouts  0.6 us

profile of v8, /device:TPU:0, one launch (start us, length us, event | category | flops | bytes accessed | tf_op | source)
XLA Modules:
  0.0 9.2 jit_solution(6300621537432524137)
XLA Ops:
  0.0 8.6 %shard_map.64 = f32[16,64]{1,0:T(8,128)S(1)} custom-call(bf16[2,3,2,128]{3,2,1,0:T(2,128)(2,1)} %sky_hbm.1, bf16[3,8,128]{2,1,0:T(8,128)(2,1)} %bitcast.3, bf16[4,8,8,128]{3,2,1,0:T(8,128)(2,1)} %bitcast.2, s32[16,256]{1,0:T(8,128)} %theta_hbm.1, s32[16,256]{1,0:T(8,128)} %phi_hbm.1, s32[16,256]{1,0:T(8,128)} %psi_hbm.1), custom_call_target="tpu_custom_call" | custom-call | tf_op jit(solution)/shard_map/pallas_call | solution.py:517
  8.6 0.6 %copy.8 = f32[16,64]{1,0:T(8,128)} copy(f32[16,64]{1,0:T(8,128)S(1)} %shard_map.64) | data formatting | bytes 8192

commit v9 on v7

--- a/solution.py
+++ b/solution.py
@@ -119,6 +119,11 @@
     def _():
         load.start()
 
+    @pl.when(jnp.logical_not(even | last))
+    def _():
+        if pushes:
+            fetch(1)
+        fetch_all()
 
     barrier = pltpu.get_barrier_semaphore()
 
@@ -133,7 +138,7 @@
     for k in range(1, n_pairs):
         greet(barrier, 2 * ((pair + k) % n_pairs), bm)
 
-    @pl.when(jnp.logical_not(ahead))
+    @pl.when(last)
     def _():
         if pushes:
             fetch(1)

time: 9.36 us -> 9.38 us (level)
  no operation moved by 1% of the time
where the time goes in v9:
time: 9.38 us; the launch traced here: 9.2 us
  Pallas kernels  8.59 us (92%)
  local copies, waits for them, and re-layouts  0.6 us (6%)
    pallas_call x1, Pallas kernels, on_device(): pl.pallas_call(functools.partial(kernel, n_det, n_bm, modes, pushes), out...  8.59 us
    unnamed x1, local copies, waits for them, and re-layouts  0.6 us

profile of v9, /device:TPU:0, one launch (start us, length us, event | category | flops | bytes accessed | tf_op | source)
XLA Modules:
  0.0 9.2 jit_solution(14417660445423279657)
XLA Ops:
  0.0 8.6 %shard_map.64 = f32[16,64]{1,0:T(8,128)S(1)} custom-call(bf16[2,3,2,128]{3,2,1,0:T(2,128)(2,1)} %sky_hbm.1, bf16[3,8,128]{2,1,0:T(8,128)(2,1)} %bitcast.3, bf16[4,8,8,128]{3,2,1,0:T(8,128)(2,1)} %bitcast.2, s32[16,256]{1,0:T(8,128)} %theta_hbm.1, s32[16,256]{1,0:T(8,128)} %phi_hbm.1, s32[16,256]{1,0:T(8,128)} %psi_hbm.1), custom_call_target="tpu_custom_call" | custom-call | tf_op jit(solution)/shard_map/pallas_call | solution.py:518
  8.6 0.6 %copy.8 = f32[16,64]{1,0:T(8,128)} copy(f32[16,64]{1,0:T(8,128)S(1)} %shard_map.64) | data formatting | bytes 8192
